TPU v7x, 32 devices: a whole 2x2x4 slice. The times are simulated.
32 devices in a mesh: fsdp: 8 (over z, x), rep: 4 (over y, core).
Axes of the slice: x: 2, y: 2, z: 4, core: 2. Of those that a mesh axis runs over, the one named last changes fastest.
Arguments:
- partials: bfloat16 [4, 56, 1024, 1024], P('rep', None, 'fsdp'), may hold values from -400 to 400
- sketch: bfloat16 [8, 4, 2, 1024, 256], P('fsdp', 'rep'), may hold values from -3 to 3
- owner_table: int32 [56, 1], replicated, may hold values from 0 to 7; in each aligned block of 14 rows (0 to 13, 14 to 27, ...) at most 2 rows name the same one
Outputs:
- update: bfloat16 [56, 1024, 1024], P('rep', 'fsdp')
- new_sketch: bfloat16 [8, 4, 2, 1024, 256], P('fsdp', 'rep')
Inputs may be any that keep to these rules, and one draw needn't show every extreme that they name: `owner_table`: in each aligned slice of 14 blocks no owner holds more than 2 blocks; some owner holds exactly 2 in some slice.
All inputs are finite; a program needn't handle non-finite values.
Results may differ from a plain program's by a relative error of at most 0.015.
Values may be sent and summed in bfloat16 or wider, within the bound.
No kernel may reach another device: no remote copies, remote signals or barrier semaphores. Data moves between devices by JAX's collectives and lax.ppermute only.
A program may use at most 128 MiB of HBM per device.

v0:
```python
import math

import jax
import jax.numpy as jnp
from jax import lax
from jax.sharding import PartitionSpec as P

NS_ITERS = 5


DECAY = 0.9
DAMPING = 64.0
FIRST_AXES = (((0,), (0,)), ((), ()))
LAST_AXES = (((1,), (1,)), ((), ()))


def inverse_root(matrix, epsilon):
    identity = jnp.eye(matrix.shape[0], dtype=jnp.float32)
    trace_sum = jnp.trace(matrix) + epsilon
    current = matrix / trace_sum
    inverse = identity
    for repeat in range(NS_ITERS):
        middle = 1.5 * identity - 0.5 * jnp.dot(inverse, current, precision=lax.Precision.HIGHEST)
        current = jnp.dot(current, middle, precision=lax.Precision.HIGHEST)
        inverse = jnp.dot(middle, inverse, precision=lax.Precision.HIGHEST)
    return inverse / jnp.sqrt(trace_sum)


def precondition(gradient, current_sketch):
    identity = jnp.eye(current_sketch.shape[1], dtype=jnp.float32)
    projected = lax.dot_general(
        gradient, current_sketch, FIRST_AXES, preferred_element_type=jnp.float32
    ).astype(jnp.bfloat16)
    gram_matrix = lax.dot_general(
        current_sketch, current_sketch, FIRST_AXES, preferred_element_type=jnp.float32
    ).astype(jnp.bfloat16)
    powered = DECAY * jnp.dot(
        current_sketch, gram_matrix, preferred_element_type=jnp.float32
    ) + jnp.dot(gradient, projected, preferred_element_type=jnp.float32)
    inner_gram = lax.dot_general(powered, powered, FIRST_AXES, precision=lax.Precision.HIGHEST)
    basis_full = jnp.dot(powered, inverse_root(inner_gram, 1e-06), precision=lax.Precision.HIGHEST)
    basis_low = basis_full.astype(jnp.bfloat16)
    coefficients = lax.dot_general(
        gradient, basis_low, FIRST_AXES, preferred_element_type=jnp.float32
    ).astype(jnp.bfloat16)
    alignment = lax.dot_general(
        current_sketch, basis_low, FIRST_AXES, preferred_element_type=jnp.float32
    )
    energy = DECAY * lax.dot_general(
        alignment, alignment, FIRST_AXES, precision=lax.Precision.HIGHEST
    ) + lax.dot_general(coefficients, coefficients, FIRST_AXES, preferred_element_type=jnp.float32)
    root_inverse = inverse_root(energy + DAMPING * identity, 0.0)
    inner_part = jnp.dot(energy, root_inverse, precision=lax.Precision.HIGHEST)
    new_block = jnp.dot(basis_full, inner_part, precision=lax.Precision.HIGHEST).astype(
        jnp.bfloat16
    )
    mix_matrix = math.sqrt(DAMPING) * root_inverse - identity
    side_terms = lax.dot_general(
        coefficients.astype(jnp.float32), mix_matrix, LAST_AXES, precision=lax.Precision.HIGHEST
    ).astype(jnp.bfloat16)
    update_block = (
        gradient.astype(jnp.float32)
        + lax.dot_general(basis_low, side_terms, LAST_AXES, preferred_element_type=jnp.float32)
    ).astype(jnp.bfloat16)
    return (update_block, new_block)


def squared_sum(values):
    wide = values.astype(jnp.float32)
    return jnp.sum(wide * wide)


def process_slot(slot_index, arrived, clip_factor, held_sketches, filled):
    block_width = arrived.shape[-1]
    gradient = (clip_factor * arrived.reshape(block_width, block_width).astype(jnp.float32)).astype(
        jnp.bfloat16
    )
    current_sketch = held_sketches[slot_index]
    active = slot_index < filled
    update_block, new_block = precondition(gradient, current_sketch)
    new_block = jnp.where(active, new_block, current_sketch)
    return (update_block, new_block)


def local(partials, sketch, owner_table):
    block_total = partials.shape[1]
    row_count = partials.shape[2]
    block_width = partials.shape[3]
    fsdp_count = lax.axis_size("fsdp")
    per_slice = block_total // lax.axis_size("rep")
    slot_count = sketch.shape[2]
    reduced = lax.psum_scatter(
        partials[0].astype(jnp.float32).astype(jnp.bfloat16), "rep", scatter_dimension=0, tiled=True
    )
    my_owners = lax.dynamic_slice_in_dim(
        owner_table[:, 0], lax.axis_index("rep") * per_slice, per_slice
    )
    positions = jnp.arange(per_slice, dtype=jnp.int32)
    same_owner = (my_owners[:, None] == my_owners[None, :]) & (
        positions[:, None] < positions[None, :]
    )
    rank_in = jnp.sum(same_owner.astype(jnp.int32), axis=0)
    target = rank_in * fsdp_count + my_owners
    selector = (
        target[None, :] == jnp.arange(slot_count * fsdp_count, dtype=jnp.int32)[:, None]
    ).astype(jnp.bfloat16)
    flattened = reduced.reshape(per_slice, row_count * block_width)
    outgoing = jnp.dot(selector, flattened, preferred_element_type=jnp.float32).astype(jnp.bfloat16)
    outgoing = outgoing.reshape(slot_count, fsdp_count, row_count, block_width)
    sum_squares = lax.psum(squared_sum(reduced), ("fsdp", "rep"))
    clip_limit = 0.5 * math.sqrt(block_total * block_width * block_width)
    clip_factor = jnp.minimum(1.0, clip_limit / jnp.sqrt(sum_squares + 1e-06))
    filled = jnp.sum((my_owners == lax.axis_index("fsdp")).astype(jnp.int32))
    held_sketches = sketch[0, 0]
    fresh_list = []
    incoming = lax.all_to_all(outgoing, "fsdp", split_axis=1, concat_axis=1, tiled=True)
    update_list = []
    for slot_index in range(slot_count):
        update_block, new_block = process_slot(
            slot_index, incoming[slot_index], clip_factor, held_sketches, filled
        )
        update_list.append(update_block)
        fresh_list.append(new_block)
    stacked = jnp.stack(update_list).reshape(slot_count, fsdp_count, row_count, block_width)
    returned = lax.all_to_all(stacked, "fsdp", split_axis=1, concat_axis=1, tiled=True)
    returned = returned.reshape(slot_count * fsdp_count, row_count * block_width)
    my_updates = lax.dot_general(
        selector, returned, FIRST_AXES, preferred_element_type=jnp.float32
    ).astype(jnp.bfloat16)
    my_updates = my_updates.reshape(per_slice, row_count, block_width)
    return (my_updates, jnp.stack(fresh_list)[None, None])


def solution(mesh):
    placed = (P("rep", None, "fsdp", None), P("fsdp", "rep", None, None, None), P())
    return jax.shard_map(
        local,
        mesh=mesh,
        in_specs=placed,
        out_specs=(P("rep", "fsdp", None), P("fsdp", "rep", None, None, None)),
        check_vma=False,
    )
```

profile of v0, /device:TPU:0, one launch (start us, length us, event | category | flops | bytes accessed | tf_op | source)
XLA Modules:
  0.0 441.3 jit_solution(7717073570326933660)
XLA Ops:
  8.8 118.5 %reduce-scatter.2.cloned.1.call-done = bf16[14,128,1024]{2,1,0:T(8,128)(2,1)} async-done(((bf16[56,128,1024]{2,1,0:T(8,128)(2,1)}), bf16[14,128,1024]{2,1,0:T(8,128)(2,1)}) %reduce-scatter.2.cloned.1.call-update) | async-done | bytes 3670032 | tf_op jit(solution)/shard_map/reduce_scatter | solution.py:92
  127.3 2.5 pad.4
  129.8 2.3 copy.28
  133.3 4.3 copy.20
  137.6 5.5 %all-to-all-start = ((bf16[2,8,128,1024]{3,2,0,1:T(8,128)(2,1)}), bf16[2,8,128,1024]{3,2,0,1:T(8,128)(2,1)}, u32[]{:S(2)}, u32[]{:S(2)}) async-start(bf16[2,8,128,1024]{3,2,0,1:T(8,128)(2,1)} %copy.20), calls=%async_computation.1 | async-start | bytes 8388608 | tf_op jit(solution)/shard_map/all_to_all | solution.py:116
  143.1 4.5 %multiply_reduce_fusion = f32[]{:T(128)} fusion(bf16[14,128,1024]{2,1,0:T(8,128)(2,1)} %reduce-scatter.2.cloned.1.call-done), kind=kLoop, calls=%fused_computation.2 | loop fusion | flops 5505023 | bytes 3670020 | tf_op jit(solution)/shard_map/reduce_sum | solution.py:70
  147.7 109.1 %psum.7 = f32[]{:T(128)} all-reduce(f32[]{:T(128)} %multiply_reduce_fusion), channel_id=1, replica_groups=mesh['fsdp'=8,'rep'=4] {'fsdp','rep'}, use_global_device_ids=true, to_apply=%region_3.0 | all-reduce | flops 1 | bytes 8 | tf_op jit(solution)/shard_map/psum | solution.py:110
  257.5 4.9 %multiply_convert_fusion.1 = (bf16[1,8,128,1024]{3,2,0,1:T(8,128)(2,1)}, bf16[1,8,128,1024]{3,2,0,1:T(8,128)(2,1)S(1)}) fusion(bf16[2,8,128,1024]{3,2,0,1:T(8,128)(2,1)} %all-to-all-done, f32[]{:T(128)S(6)} %min_shard_map.3), kind=kLoop, calls=%fused_computation.8 | loop fusion | flops 6291456 | bytes 8388612 | tf_op jit(solution)/shard_map/convert_element_type | solution.py:75
  263.7 3.3 fusion.11
  267.0 2.1 fusion.1
  269.1 1.6 select_reduce_fusion.1
  276.7 1.8 fusion.92
  289.2 5.5 %fusion.10 = f32[1024,256]{0,1:T(8,128)} fusion(bf16[1024,1024]{1,0:T(8,128)(2,1)} %bitcast.197, bf16[1,1,2,1024,256]{4,3,2,1,0:T(8,128)(2,1)S(1)} %copy-done), kind=kOutput, calls=%fused_computation.77 | convolution fusion | flops 1074003968 | bytes 5767168 | tf_op jit(solution)/shard_map/dot_general | solution.py:39
  294.7 2.1 fusion.3
  296.8 2.4 select_reduce_fusion.3
  307.3 1.8 fusion.78
  323.3 2.3 pad_maximum_fusion
  325.7 4.7 %all-to-all-start.1 = ((bf16[2,8,128,1024]{3,2,0,1:T(8,128)(2,1)}), bf16[2,8,128,1024]{3,2,0,1:T(8,128)(2,1)}, u32[]{:S(2)}, u32[]{:S(2)}) async-start(bf16[2,8,128,1024]{3,2,0,1:T(8,128)(2,1)} %pad_maximum_fusion), calls=%async_computation.2 | async-start | bytes 8388608 | tf_op jit(solution)/shard_map/all_to_all | solution.py:125
  337.6 85.4 %all-to-all-done.1 = bf16[2,8,128,1024]{3,2,0,1:T(8,128)(2,1)} async-done(((bf16[2,8,128,1024]{3,2,0,1:T(8,128)(2,1)}), bf16[2,8,128,1024]{3,2,0,1:T(8,128)(2,1)}, u32[]{:S(2)}, u32[]{:S(2)}) %all-to-all-start.1) | async-done | bytes 4194336 | tf_op jit(solution)/shard_map/all_to_all | solution.py:125
  423.0 2.6 copy.32
  425.6 2.3 copy.29
  428.0 1.5 convolution_convert_fusion
  429.5 2.3 copy.30
  431.8 2.2 slice.20
  (118 shorter events, 45.6 us)
Async XLA Ops:
  7.2 120.1 %reduce-scatter.2.cloned.1.call-start = ((), (), s32[]{:S(2)}) async-start(), calls=%async_computation.3 | async-start | bytes 18350080 | tf_op jit(solution)/shard_map/reduce_scatter | solution.py:92
  7.2 0.7 copy-start.18
  137.6 119.8 %all-to-all-start = ((bf16[2,8,128,1024]{3,2,0,1:T(8,128)(2,1)}), bf16[2,8,128,1024]{3,2,0,1:T(8,128)(2,1)}, u32[]{:S(2)}, u32[]{:S(2)}) async-start(bf16[2,8,128,1024]{3,2,0,1:T(8,128)(2,1)} %copy.20), calls=%async_computation.1 | async-start | bytes 8388608 | tf_op jit(solution)/shard_map/all_to_all | solution.py:116
  257.4 6.3 %copy-start = (bf16[1,1,2,1024,256]{4,3,2,1,0:T(8,128)(2,1)S(1)}, bf16[1,1,2,1024,256]{4,3,2,1,0:T(8,128)(2,1)}, u32[]{:S(2)}) copy-start(bf16[1,1,2,1024,256]{4,3,2,1,0:T(8,128)(2,1)} %param.4) | copy-start | bytes 3145732
  262.4 1.3 copy-start.5
  274.7 4.1 copy-start.6
  279.8 0.8 copy-start.8
  282.0 5.7 %copy-start.16 = (f32[256,256]{1,0:T(8,128)}, f32[256,256]{1,0:T(8,128)S(1)}, u32[]{:S(2)}) copy-start(f32[256,256]{1,0:T(8,128)S(1)} %get-tuple-element.9) | copy-start | bytes 786436
  305.1 4.3 copy-start.3
  309.1 1.5 copy-start.1
  310.2 1.4 copy-start.10
  311.6 5.5 %copy-start.17 = (f32[256,256]{1,0:T(8,128)}, f32[256,256]{1,0:T(8,128)S(1)}, u32[]{:S(2)}) copy-start(f32[256,256]{1,0:T(8,128)S(1)} %get-tuple-element.13) | copy-start | bytes 786436
  313.1 4.8 %copy-start.12 = (f32[256,256]{1,0:T(8,128)S(1)}, f32[256,256]{1,0:T(8,128)}, u32[]{:S(2)}) copy-start(f32[256,256]{1,0:T(8,128)} %fusion.99) | copy-start | bytes 786436
  314.8 4.6 %copy-start.9 = (bf16[1024,256]{1,0:T(8,128)(2,1)S(1)}, bf16[1024,256]{1,0:T(8,128)(2,1)}, u32[]{:S(2)}) copy-start(bf16[1024,256]{1,0:T(8,128)(2,1)} %copy-done.8) | copy-start | bytes 1572868
  315.2 4.9 %copy-start.7 = (bf16[1,8,128,1024]{3,2,0,1:T(8,128)(2,1)S(1)}, bf16[1,8,128,1024]{3,2,0,1:T(8,128)(2,1)}, u32[]{:S(2)}) copy-start(bf16[1,8,128,1024]{3,2,0,1:T(8,128)(2,1)} %copy-done.5) | copy-start | bytes 6291460
  318.7 0.7 copy-start.13
  319.4 2.2 copy-start.11
  320.1 2.5 copy-start.2
  320.1 2.5 copy-start.4
  321.7 1.7 copy-start.15
  325.7 6.1 %copy-start.14 = (f32[256,256]{1,0:T(8,128)S(1)}, f32[256,256]{1,0:T(8,128)}, u32[]{:S(2)}) copy-start(f32[256,256]{1,0:T(8,128)} %copy-done.13) | copy-start | bytes 786436
  325.7 97.3 %all-to-all-start.1 = ((bf16[2,8,128,1024]{3,2,0,1:T(8,128)(2,1)}), bf16[2,8,128,1024]{3,2,0,1:T(8,128)(2,1)}, u32[]{:S(2)}, u32[]{:S(2)}) async-start(bf16[2,8,128,1024]{3,2,0,1:T(8,128)(2,1)} %pad_maximum_fusion), calls=%async_computation.2 | async-start | bytes 8388608 | tf_op jit(solution)/shard_map/all_to_all | solution.py:125
Sparse Core Ops, SparseCore 0:
  10.6 116.6 reduce-scatter.1
where the time goes:
time: 448 us; the launch traced here: 441 us
  waiting for transfers between devices  205 us (46%)
  blocking collectives  109 us (24%)
  matrix products  61.9 us (14%)
  local copies, waits for them, and re-layouts  21.8 us (5%)
  between operations  20.1 us (4%)
  other arithmetic  13.8 us (3%)
  starting transfers between devices  10.2 us (2%)
    reduce_scatter x1, waiting for transfers between devices, local(): lax.psum_scatter(partials[0].astype(jnp.float32).astype(jnp.bfloat16), 'r...  118 us
    psum x1, blocking collectives, local(): sum_squares = lax.psum(squared_sum(reduced), ('fsdp', 'rep'))  109 us
    all_to_all x1, waiting for transfers between devices, local(): lax.all_to_all(stacked, 'fsdp', split_axis=1, concat_axis=1, tiled=True)  85.4 us
    unnamed x42, local copies, waits for them, and re-layouts  12.6 us
    dot_general x20, matrix products, inverse_root(): jnp.dot(inverse, current, precision=lax.Precision.HIGHEST)  9.76 us
    dot_general x16, matrix products, inverse_root(): current = jnp.dot(current, middle, precision=lax.Precision.HIGHEST)  9 us
  transfers between devices with their start and end apart: 3, of which 2 were waited for; matrix products, arithmetic and copies ran while one was open for 3% of the time, Pallas kernels for 0%

commit v1 on v0

v1 whole, which is shorter than its diff:
```python
import math

import jax
import jax.numpy as jnp
from jax import lax
from jax.experimental import pallas as pl
from jax.experimental.pallas import tpu as pltpu
from jax.sharding import PartitionSpec as P


NS_ITERS = 5
DECAY = 0.9
DAMPING = 64.0
CORES = 2
PARTS = 2
NN = (((1,), (0,)), ((), ()))
NT = (((1,), (1,)), ((), ()))


def dot(left, right, dims=NN):
    return lax.dot_general(left, right, dims, preferred_element_type=jnp.float32)


def split(value):
    high = value.astype(jnp.bfloat16)
    return high, (value - high.astype(jnp.float32)).astype(jnp.bfloat16)


def dot3(left, right, dims=NN):
    return dot(left[0], right[0], dims) + (
        dot(left[0], right[1], dims) + dot(left[1], right[0], dims)
    )


def diagonal(size):
    rows = lax.broadcasted_iota(jnp.int32, (size, size), 0)
    return rows == lax.broadcasted_iota(jnp.int32, (size, size), 1)


def inverse_root(matrix, epsilon):
    on_diagonal = diagonal(matrix.shape[0])
    trace_sum = jnp.sum(jnp.where(on_diagonal, matrix, 0.0), axis=(0, 1), keepdims=True) + epsilon
    current = matrix / trace_sum
    three_halves = jnp.where(on_diagonal, 1.5, 0.0)
    middle = three_halves - 0.5 * current
    inverse = middle
    middle_pair = split(middle)
    current_pair = split(current)
    for _ in range(1, NS_ITERS):
        current_pair = split(dot3(current_pair, middle_pair))
        inverse_pair = split(inverse)
        middle = three_halves - 0.5 * dot3(inverse_pair, current_pair)
        middle_pair = split(middle)
        inverse = dot3(middle_pair, inverse_pair)
    return inverse * lax.rsqrt(trace_sum)


def precondition_kernel(slot_ref, clip_ref, sketch_ref, *rest):
    *arrived_refs, update_ref, new_ref, gradient_ref = rest
    clip = clip_ref[0, 0]
    for number, piece_ref in enumerate(arrived_refs):
        across = piece_ref.shape[1]
        gradient_ref[:, number * across : (number + 1) * across] = (
            piece_ref[...].astype(jnp.float32) * clip
        ).astype(jnp.bfloat16)
    held = sketch_ref[slot_ref[0]]
    rank = held.shape[1]
    held_t = held.T
    projected_t = dot(held_t, gradient_ref[...]).astype(jnp.bfloat16)
    gram = dot(held_t, held).astype(jnp.bfloat16)
    powered_t = DECAY * dot(gram, held_t) + dot(projected_t, gradient_ref[...], NT)
    powered_pair = split(powered_t)
    root = inverse_root(dot3(powered_pair, powered_pair, NT), 1e-06)
    basis_t = dot3(split(root), powered_pair)
    basis_pair = split(basis_t)
    basis_low_t = basis_pair[0]
    coefficients_t = dot(basis_low_t, gradient_ref[...]).astype(jnp.bfloat16)
    alignment_pair = split(dot(basis_low_t, held))
    energy = DECAY * dot3(alignment_pair, alignment_pair, NT) + dot(
        coefficients_t, coefficients_t, NT
    )
    on_diagonal = diagonal(rank)
    root_inverse = inverse_root(energy + jnp.where(on_diagonal, DAMPING, 0.0), 0.0)
    mix = math.sqrt(DAMPING) * root_inverse - jnp.where(on_diagonal, 1.0, 0.0)
    mix_pair = split(mix)
    side_t = (dot(mix_pair[0], coefficients_t) + dot(mix_pair[1], coefficients_t)).astype(
        jnp.bfloat16
    )
    update_ref[...] = (
        gradient_ref[...].astype(jnp.float32) + dot(basis_low_t.T, side_t)
    ).astype(jnp.bfloat16)
    inner = dot3(split(root_inverse), split(energy))
    new_ref[...] = dot3(split(inner), basis_pair).astype(jnp.bfloat16).T


def precondition(slot, clip, arrived, held):
    width, rank = held.shape[1:]
    return pl.pallas_call(
        precondition_kernel,
        out_shape=(
            jax.ShapeDtypeStruct((width, width), jnp.bfloat16),
            jax.ShapeDtypeStruct((width, rank), jnp.bfloat16),
        ),
        in_specs=[
            pl.BlockSpec(memory_space=pltpu.SMEM),
            pl.BlockSpec(memory_space=pltpu.SMEM),
            *[pl.BlockSpec(memory_space=pltpu.VMEM)] * (1 + len(arrived)),
        ],
        out_specs=(
            pl.BlockSpec(memory_space=pltpu.VMEM),
            pl.BlockSpec(memory_space=pltpu.VMEM),
        ),
        scratch_shapes=[pltpu.VMEM((width, width), jnp.bfloat16)],
        compiler_params=pltpu.CompilerParams(vmem_limit_bytes=48 * 2**20),
        cost_estimate=pl.CostEstimate(
            flops=24 * width * width * rank, bytes_accessed=6 * width * width, transcendentals=0
        ),
        name="precondition",
    )(slot, clip, held, *arrived)


class Piece:
    def __init__(self, start, count, part, parts, per_slice, partial, source):
        self.start, self.count, self.per_slice = start, count, per_slice
        self.partial, self.source = partial, source
        self.rows, self.width = partial.shape[1], partial.shape[2] // parts
        self.first_column = part * self.width
        self.shape = jax.ShapeDtypeStruct((count, self.rows, self.width), partial.dtype)

    def copies(self, which, source_ref, slices_ref, partial_ref, held_ref, semaphores):
        base = slices_ref[which] * self.per_slice + self.start
        columns = pl.ds(self.first_column, self.width)
        return [
            pltpu.make_async_copy(
                partial_ref.at[source_ref[base + at], :, columns], held_ref.at[at], semaphores.at[at]
            )
            for at in range(self.count)
        ]

    def call(self, kernel, slices, operands, out_shape, scalars=()):
        return pl.pallas_call(
            kernel,
            out_shape=out_shape,
            in_specs=[pl.BlockSpec(memory_space=pltpu.SMEM)] * (2 + len(scalars))
            + [pl.BlockSpec(memory_space=pl.ANY)]
            + [pl.BlockSpec(memory_space=pltpu.VMEM)] * len(operands),
            out_specs=jax.tree.map(lambda _: pl.BlockSpec(memory_space=pltpu.VMEM), out_shape),
            scratch_shapes=[
                pltpu.VMEM(self.shape.shape, self.shape.dtype),
                pltpu.SemaphoreType.DMA((self.count,)),
            ],
        )(self.source, slices, *scalars, self.partial, *operands)

    def add(self, which, slices, other):
        def kernel(source_ref, slices_ref, partial_ref, other_ref, out_ref, held_ref, semaphores):
            copies = self.copies(which, source_ref, slices_ref, partial_ref, held_ref, semaphores)
            for copy in copies:
                copy.start()
            for at, copy in enumerate(copies):
                copy.wait()
                total = held_ref[at].astype(jnp.float32) + other_ref[at].astype(jnp.float32)
                out_ref[at] = total.astype(out_ref.dtype)

        return self.call(kernel, slices, [other], self.shape)

    def total(self, which, slices, others, index, valid):
        owners = index.shape[0]

        def kernel(source_ref, slices_ref, index_ref, valid_ref, partial_ref, *rest):
            *other_refs, out_ref, square_ref, held_ref, semaphores = rest
            copies = self.copies(which, source_ref, slices_ref, partial_ref, held_ref, semaphores)
            for copy in copies:
                copy.start()
            for copy in copies:
                copy.wait()
            square_ref[...] = jnp.zeros_like(square_ref)

            @pl.loop(0, owners)
            def _(owner):
                at = index_ref[owner]
                total = held_ref[at].astype(jnp.float32)
                for other_ref in other_refs:
                    total = total + other_ref[at].astype(jnp.float32)
                rounded = total.astype(out_ref.dtype)
                out_ref[owner] = rounded
                wide = rounded.astype(jnp.float32)
                squares = jnp.sum((wide * wide).reshape(-1, 8, wide.shape[-1]), axis=0)
                square_ref[...] += jnp.where(valid_ref[owner] > 0, squares, 0.0)

        out_shape = (
            jax.ShapeDtypeStruct((owners, self.rows, self.width), self.partial.dtype),
            jax.ShapeDtypeStruct((8, self.width), jnp.float32),
        )
        return self.call(kernel, slices, others, out_shape, (index, valid))


def pick_blocks(pieces, which, slices):
    counts = [piece.count for piece in pieces]

    def kernel(source_ref, slices_ref, partial_ref, *rest):
        *out_refs, semaphores = rest
        copies = [
            copy
            for number, (piece, out_ref) in enumerate(zip(pieces, out_refs))
            for copy in piece.copies(
                which, source_ref, slices_ref, partial_ref, out_ref, semaphores.at[number]
            )
        ]
        for copy in copies:
            copy.start()
        for copy in copies:
            copy.wait()

    return pl.pallas_call(
        kernel,
        out_shape=[piece.shape for piece in pieces],
        in_specs=[pl.BlockSpec(memory_space=pltpu.SMEM)] * 2 + [pl.BlockSpec(memory_space=pl.ANY)],
        out_specs=[pl.BlockSpec(memory_space=pltpu.VMEM) for _ in pieces],
        scratch_shapes=[pltpu.SemaphoreType.DMA((len(pieces), max(counts)))],
        name="pick_blocks",
    )(pieces[0].source, slices, pieces[0].partial)


def place_kernel(source_index_ref, target_index_ref, source_ref, *rest):
    out_ref, semaphores = rest[-2:]
    copies = [
        pltpu.make_async_copy(
            source_ref.at[source_index_ref[at]], out_ref.at[target_index_ref[at]], semaphores.at[at]
        )
        for at in range(semaphores.shape[0])
    ]
    for copy in copies:
        copy.start()
    for copy in copies:
        copy.wait()


def place_blocks(source_index, target_index, source, total, onto=None):
    smem = pl.BlockSpec(memory_space=pltpu.SMEM)
    anywhere = pl.BlockSpec(memory_space=pl.ANY)
    onto_list = [] if onto is None else [onto]
    return pl.pallas_call(
        place_kernel,
        in_specs=[smem, smem, pl.BlockSpec(memory_space=pltpu.VMEM)] + [anywhere] * len(onto_list),
        out_specs=anywhere,
        out_shape=jax.ShapeDtypeStruct((total,) + source.shape[1:], source.dtype),
        scratch_shapes=[pltpu.SemaphoreType.DMA(source_index.shape)],
        input_output_aliases={3: 0} if onto_list else {},
        name="place_blocks",
    )(source_index, target_index, source, *onto_list)


def total_over(value, axis):
    size = lax.axis_size(axis)
    if size & (size - 1):
        return lax.psum(value, axis)
    spread = jnp.full((8, 128), value)
    apart = 1
    while apart < size:
        spread = spread + lax.ppermute(spread, axis, [(at, at ^ apart) for at in range(size)])
        apart *= 2
    return spread[0, 0]


def local(partials, sketch, owner_table):
    block_total, row_count, block_width = partials.shape[1:]
    fsdp_count = lax.axis_size("fsdp")
    rep_count = lax.axis_size("rep")
    per_slice = block_total // rep_count
    held_sketches = sketch[0, 0]
    half_sizes = ((per_slice + 1) // 2, per_slice // 2)
    half_starts = (0, half_sizes[0])

    owners = owner_table[:, 0].reshape(rep_count, per_slice)
    places = jnp.arange(per_slice, dtype=jnp.int32)
    before = (places[:, None] < places[None, :])[None]
    same = owners[:, :, None] == owners[:, None, :]
    alone = jnp.sum(same.astype(jnp.int32), axis=1) == 1
    rank_in = jnp.sum((same & before).astype(jnp.int32), axis=1)
    alone_rank = jnp.sum((alone[:, :, None] & before).astype(jnp.int32), axis=1)
    alone_count = jnp.sum(alone.astype(jnp.int32), axis=1, keepdims=True)
    half = jnp.where(alone, (2 * alone_rank >= alone_count).astype(jnp.int32), rank_in)
    in_half = jnp.sum(((half[:, :, None] == half[:, None, :]) & before).astype(jnp.int32), axis=1)
    target = half * half_sizes[0] + in_half
    order = jnp.sum(
        jnp.where(target[:, :, None] == places[None, None, :], places[None, :, None], 0), axis=1
    )
    source = order + per_slice * jnp.arange(rep_count, dtype=jnp.int32)[:, None]

    my_slice = lax.axis_index("rep")
    my_owners, my_half, my_in_half, my_order = (
        lax.dynamic_index_in_dim(value, my_slice, 0, keepdims=False)
        for value in (owners, half, in_half, order)
    )
    owner_ids = jnp.arange(fsdp_count, dtype=jnp.int32)
    mine = my_owners == lax.axis_index("fsdp")
    both = jnp.sum(mine.astype(jnp.int32)) > 1

    partial = partials[0]
    outer_count = rep_count // CORES
    my_outer, my_core = my_slice // CORES, my_slice % CORES
    outers = (my_outer + jnp.arange(outer_count, dtype=jnp.int32)) % outer_count
    slices = jnp.concatenate([outers * CORES + (CORES - 1 - my_core), outers * CORES + my_core])
    source = source.reshape(-1)
    swap = [(at, at ^ 1) for at in range(rep_count)]

    pieces = [
        Piece(half_starts[number], half_sizes[number], part, PARTS, per_slice, partial, source)
        for number in range(2)
        for part in range(PARTS)
    ]
    others = [[] for _ in pieces]
    for step in range(1, outer_count):
        onward = [(at, (at + step * CORES) % rep_count) for at in range(rep_count)]
        picked = pick_blocks(pieces[:1], step, slices)
        later_slices, picked = lax.optimization_barrier((slices, picked))
        picked = picked + pick_blocks(pieces[1:], step, later_slices)
        for piece, sent, gathered in zip(pieces, picked, others):
            crossed = lax.ppermute(sent, "rep", swap)
            summed = piece.add(outer_count + step, later_slices, crossed)
            gathered.append(lax.ppermute(summed, "rep", onward))
            later_slices, _ = lax.optimization_barrier((later_slices, summed))
        slices = later_slices
    own = pick_blocks(pieces, 0, slices)
    for gathered, sent in zip(others, own):
        gathered.append(lax.ppermute(sent, "rep", swap))

    arrived, sums, clip_factor = [], [], None
    for number, (piece, gathered) in enumerate(zip(pieces, others)):
        holds = (my_owners[:, None] == owner_ids[None, :]) & (my_half[:, None] == number // PARTS)
        index = jnp.sum(jnp.where(holds, my_in_half[:, None], 0), axis=0)
        valid = jnp.sum(holds.astype(jnp.int32), axis=0)
        if number >= 2:
            gathered[0], arrived[number - 2] = lax.optimization_barrier(
                (gathered[0], arrived[number - 2])
            )
        laid_out, square = piece.total(outer_count, slices, gathered, index, valid)
        sums.append(jnp.sum(square))
        if number == len(pieces) - 1:
            sum_squares = total_over(total_over(sum(sums), "rep"), "fsdp")
            clip_limit = 0.5 * math.sqrt(block_total * block_width * block_width)
            clip_factor = jnp.minimum(1.0, clip_limit / jnp.sqrt(sum_squares + 1e-06))
            laid_out, clip_factor = lax.optimization_barrier((laid_out, clip_factor))
        got = lax.all_to_all(laid_out, "fsdp", split_axis=0, concat_axis=0, tiled=True)
        arrived.append(got.reshape(block_width, -1))
    arrived = (arrived[:PARTS], arrived[PARTS:])
    clip = clip_factor.reshape(1, 1)

    updates, fresh = None, []
    slots = (jnp.zeros((1,), jnp.int32), both.astype(jnp.int32).reshape(1))
    for number in range(2):
        start, size = half_starts[number], half_sizes[number]
        update, new_block = precondition(
            slots[number], clip, arrived[number], held_sketches
        )
        fresh.append(new_block)
        returned = lax.all_to_all(
            update.reshape(fsdp_count, row_count, block_width),
            "fsdp",
            split_axis=0,
            concat_axis=0,
            tiled=True,
        )
        targets = my_order[start : start + size]
        owners_here = jnp.sum(
            jnp.where(targets[:, None] == places[None, :], my_owners[None, :], 0), axis=1
        )
        updates = place_blocks(owners_here, targets, returned, per_slice, updates)
    has_first = jnp.sum((mine & (my_half == 0)).astype(jnp.int32)) > 0
    has_second = jnp.sum((mine & (my_half == 1)).astype(jnp.int32)) > 0
    slot_zero = jnp.where(
        has_first, fresh[0], jnp.where(has_second, fresh[1], held_sketches[0])
    )
    slot_one = jnp.where(both, fresh[1], held_sketches[1])
    return (updates, jnp.stack([slot_zero, slot_one])[None, None])


def solution(mesh):
    placed = (P("rep", None, "fsdp", None), P("fsdp", "rep", None, None, None), P())
    return jax.shard_map(
        local,
        mesh=mesh,
        in_specs=placed,
        out_specs=(P("rep", "fsdp", None), P("fsdp", "rep", None, None, None)),
        check_vma=False,
    )
```

time: 448 us -> 289 us (0.65); the launches traced: 441 us -> 287 us
  blocking collectives: 109 us -> 0 us
  Pallas kernels: 0 us -> 77.2 us
  waiting for transfers between devices: 205 us -> 135 us
  matrix products: 61.9 us -> 0 us
  starting transfers between devices: 10.2 us -> 48.8 us
  between operations: 20.1 us -> 6.42 us
  local copies, waits for them, and re-layouts: 21.8 us -> 9.14 us
    reduce_scatter x1 -> x0, waiting for transfers between devices: 118 us -> none  [local(): lax.psum_scatter(partials[0].astype(jnp.float32).astype(jnp.bfloat16), 'r...]
    psum x1 -> x0, blocking collectives: 109 us -> none  [local(): sum_squares = lax.psum(squared_sum(reduced), ('fsdp', 'rep'))]
    pallas_call x0 -> x15, Pallas kernels: none -> 77.2 us  [the longest x8 31.5 us: call(): pl.pallas_call(kernel, out_shape=out_shape, in_specs=[pl.BlockSpec(memory...]
    dot_general x82 -> x0, matrix products: 61.9 us -> none  [the longest x20 9.76 us: inverse_root(): jnp.dot(inverse, current, precision=lax.Precision.HIGHEST)]
    ppermute x0 -> x17, waiting for transfers between devices: none -> 55 us  [the longest x4 46.2 us: local(): gathered.append(lax.ppermute(summed, 'rep', onward))]
    all_to_all x2 -> x6, starting transfers between devices: 10.2 us -> 32.8 us  [the longest x4 23.7 us: local(): lax.all_to_all(laid_out, 'fsdp', split_axis=0, concat_axis=0, tiled=True)]
    ppermute x0 -> x17, starting transfers between devices: none -> 16 us  [the longest x5 7.91 us: total_over(): lax.ppermute(spread, axis, [(at, at ^ apart) for at in range(size)])]
    reshape x2 -> x0, local copies, waits for them, and re-layouts: 6.51 us -> none  [the longest x1 4.3 us: local(): outgoing = outgoing.reshape(slot_count, fsdp_count, row_count, block_width)]
  transfers between devices with their start and end apart: 3 -> 23, of which waited for: 2 -> 12; matrix products, arithmetic and copies ran while one was open for 3% -> 3% of each run, Pallas kernels for 0% -> 23%
where the time goes in v1:
time: 289 us; the launch traced here: 287 us
  waiting for transfers between devices  135 us (47%)
  Pallas kernels  77.2 us (27%)
  starting transfers between devices  48.8 us (17%)
  other arithmetic  10.6 us (4%)
  local copies, waits for them, and re-layouts  9.14 us (3%)
  between operations  6.42 us (2%)
    all_to_all x2, waiting for transfers between devices, local(): lax.all_to_all(update.reshape(fsdp_count, row_count, block_width), 'fsdp'...  72.1 us
    ppermute x4, waiting for transfers between devices, local(): gathered.append(lax.ppermute(summed, 'rep', onward))  46.2 us
    pallas_call x8, Pallas kernels, call(): pl.pallas_call(kernel, out_shape=out_shape, in_specs=[pl.BlockSpec(memory...  31.5 us
    pallas_call x2, Pallas kernels, precondition(): pl.pallas_call(precondition_kernel, out_shape=(jax.ShapeDtypeStruct((widt...  27.9 us
    all_to_all x4, starting transfers between devices, local(): lax.all_to_all(laid_out, 'fsdp', split_axis=0, concat_axis=0, tiled=True)  23.7 us
    pallas_call x3, Pallas kernels, pick_blocks(): pl.pallas_call(kernel, out_shape=[piece.shape for piece in pieces], in_sp...  11.9 us
    all_to_all x2, starting transfers between devices, local(): lax.all_to_all(update.reshape(fsdp_count, row_count, block_width), 'fsdp'...  9.03 us
    ppermute x5, waiting for transfers between devices, total_over(): lax.ppermute(spread, axis, [(at, at ^ apart) for at in range(size)])  8.84 us
  transfers between devices with their start and end apart: 23, of which 12 were waited for; matrix products, arithmetic and copies ran while one was open for 3% of the time, Pallas kernels for 23%

profile of v1, /device:TPU:0, one launch (start us, length us, event | category | flops | bytes accessed | tf_op | source)
XLA Modules:
  0.0 287.2 jit_solution(450494568889493152)
XLA Ops:
  8.4 4.2 %pick_blocks.4 = (bf16[7,128,512]{2,1,0:T(8,128)(2,1)}, bf16[7,128,512]{2,1,0:T(8,128)(2,1)}, bf16[7,128,512]{2,1,0:T(8,128)(2,1)}) custom-call(s32[56]{0:T(128)} %add.87.source_ref, s32[4]{0:T(128)} %pad_add_fusion.slices_ref, bf16[56,128,1024]{2,1,0:T(8,128)(2,1)} %bitcast.49), custom_call_target="tpu_custom_call" | custom-call | tf_op jit(solution)/shard_map/pick_blocks/pallas_call | solution.py:214
  14.2 3.5 %shard_map.50 = bf16[7,128,512]{2,1,0:T(8,128)(2,1)} custom-call(s32[56]{0:T(128)} %add.87.source_ref, s32[4]{0:T(128)} %pad_add_fusion.slices_ref, bf16[56,128,1024]{2,1,0:T(8,128)(2,1)} %bitcast.50, bf16[7,128,512]{2,1,0:T(8,128)(2,1)} %copy-done.9), custom_call_target="tpu_custom_call" | custom-call | tf_op jit(solution)/shard_map/pallas_call | solution.py:141
  20.7 3.4 %shard_map.51 = bf16[7,128,512]{2,1,0:T(8,128)(2,1)} custom-call(s32[56]{0:T(128)} %add.87.source_ref, s32[4]{0:T(128)} %pad_add_fusion.slices_ref, bf16[56,128,1024]{2,1,0:T(8,128)(2,1)} %bitcast.51, bf16[7,128,512]{2,1,0:T(8,128)(2,1)} %collective-permute-done.1.other_ref), custom_call_target="tpu_custom_call" | custom-call | tf_op jit(solution)/shard_map/pallas_call | solution.py:141
  25.1 3.5 %shard_map.52 = bf16[7,128,512]{2,1,0:T(8,128)(2,1)} custom-call(s32[56]{0:T(128)} %add.87.source_ref, s32[4]{0:T(128)} %pad_add_fusion.slices_ref, bf16[56,128,1024]{2,1,0:T(8,128)(2,1)} %bitcast.52, bf16[7,128,512]{2,1,0:T(8,128)(2,1)} %copy-done.8), custom_call_target="tpu_custom_call" | custom-call | tf_op jit(solution)/shard_map/pallas_call | solution.py:141
  29.5 3.5 %shard_map.53 = bf16[7,128,512]{2,1,0:T(8,128)(2,1)} custom-call(s32[56]{0:T(128)} %add.87.source_ref, s32[4]{0:T(128)} %pad_add_fusion.slices_ref, bf16[56,128,1024]{2,1,0:T(8,128)(2,1)} %bitcast.53, bf16[7,128,512]{2,1,0:T(8,128)(2,1)} %copy-done.7), custom_call_target="tpu_custom_call" | custom-call | tf_op jit(solution)/shard_map/pallas_call | solution.py:141
  33.0 4.8 %pick_blocks.5 = (bf16[7,128,512]{2,1,0:T(8,128)(2,1)}, bf16[7,128,512]{2,1,0:T(8,128)(2,1)}, bf16[7,128,512]{2,1,0:T(8,128)(2,1)}, bf16[7,128,512]{2,1,0:T(8,128)(2,1)}) custom-call(s32[56]{0:T(128)} %add.87.source_ref, s32[4]{0:T(128)} %pad_add_fusion.slices_ref, bf16[56,128,1024]{2,1,0:T(8,128)(2,1)} %bitcast.54), custom_call_target="tpu_custom_call" | custom-call | tf_op jit(solution)/shard_map/pick_blocks/pallas_call | solution.py:214
  42.7 4.4 %shard_map.56 = (bf16[8,128,512]{2,1,0:T(8,128)(2,1)}, f32[8,512]{1,0:T(8,128)}) custom-call(s32[56]{0:T(128)} %add.87.source_ref, s32[4]{0:T(128)} %pad_add_fusion.slices_ref, s32[8]{0:T(128)} %get-tuple-element.67.index_ref, s32[8]{0:T(128)} %get-tuple-element.66.valid_ref, bf16[56,128,1024]{2,1,0:T(8,128)(2,1)} %bitcast.55, ...), custom_call_target="tpu_custom_call" | custom-call | tf_op jit(solution)/shard_map/pallas_call | solution.py:141
  47.2 6.2 %all-to-all-start.1 = ((bf16[8,128,512]{2,1,0:T(8,128)(2,1)}), bf16[8,128,512]{2,1,0:T(8,128)(2,1)S(1)}, u32[]{:S(2)}, u32[]{:S(2)}) async-start(bf16[8,128,512]{2,1,0:T(8,128)(2,1)} %get-tuple-element.50), calls=%async_computation.1 | async-start | bytes 2097152 | tf_op jit(solution)/shard_map/all_to_all | solution.py:344
  54.9 19.7 %collective-permute-done.5.rest_0_ = bf16[7,128,512]{2,1,0:T(8,128)(2,1)S(1)} collective-permute-done((bf16[7,128,512]{2,1,0:T(8,128)(2,1)S(1)}, bf16[7,128,512]{2,1,0:T(8,128)(2,1)S(1)}, u32[]{:S(2)}, u32[]{:S(2)}) %collective-permute-start.5) | collective-permute-done | bytes 917536 | tf_op jit(solution)/shard_map/ppermute | solution.py:321
  75.5 4.4 %shard_map.54 = (bf16[8,128,512]{2,1,0:T(8,128)(2,1)}, f32[8,512]{1,0:T(8,128)}) custom-call(s32[56]{0:T(128)} %add.87.source_ref, s32[4]{0:T(128)} %pad_add_fusion.slices_ref, s32[8]{0:T(128)} %get-tuple-element.67.index_ref, s32[8]{0:T(128)} %get-tuple-element.66.valid_ref, bf16[56,128,1024]{2,1,0:T(8,128)(2,1)} %bitcast.56, ...), custom_call_target="tpu_custom_call" | custom-call | tf_op jit(solution)/shard_map/pallas_call | solution.py:141
  80.0 5.8 %all-to-all-start = ((bf16[8,128,512]{2,1,0:T(8,128)(2,1)}), bf16[8,128,512]{2,1,0:T(8,128)(2,1)S(1)}, u32[]{:S(2)}, u32[]{:S(2)}) async-start(bf16[8,128,512]{2,1,0:T(8,128)(2,1)} %get-tuple-element.43), calls=%async_computation | async-start | bytes 2097152 | tf_op jit(solution)/shard_map/all_to_all | solution.py:344
  88.0 21.3 %collective-permute-done.10.rest_0_ = bf16[7,128,512]{2,1,0:T(8,128)(2,1)} collective-permute-done((bf16[7,128,512]{2,1,0:T(8,128)(2,1)}, bf16[7,128,512]{2,1,0:T(8,128)(2,1)}, u32[]{:S(2)}, u32[]{:S(2)}) %collective-permute-start.10) | collective-permute-done | bytes 917536 | tf_op jit(solution)/shard_map/ppermute | solution.py:321
  109.3 4.4 %shard_map.57 = (bf16[8,128,512]{2,1,0:T(8,128)(2,1)}, f32[8,512]{1,0:T(8,128)}) custom-call(s32[56]{0:T(128)} %add.87.source_ref, s32[4]{0:T(128)} %pad_add_fusion.slices_ref, s32[8]{0:T(128)} %get-tuple-element.68.index_ref, s32[8]{0:T(128)} %get-tuple-element.69.valid_ref, bf16[56,128,1024]{2,1,0:T(8,128)(2,1)} %bitcast.57, ...), custom_call_target="tpu_custom_call" | custom-call | tf_op jit(solution)/shard_map/pallas_call | solution.py:141
  113.8 6.0 %all-to-all-start.2 = ((bf16[8,128,512]{2,1,0:T(8,128)(2,1)}), bf16[8,128,512]{2,1,0:T(8,128)(2,1)}, u32[]{:S(2)}, u32[]{:S(2)}) async-start(bf16[8,128,512]{2,1,0:T(8,128)(2,1)} %get-tuple-element.56), calls=%async_computation.2 | async-start | bytes 2097152 | tf_op jit(solution)/shard_map/all_to_all | solution.py:344
  122.4 3.1 %collective-permute-done.4.rest_0_ = bf16[7,128,512]{2,1,0:T(8,128)(2,1)} collective-permute-done((bf16[7,128,512]{2,1,0:T(8,128)(2,1)S(1)}, bf16[7,128,512]{2,1,0:T(8,128)(2,1)}, u32[]{:S(2)}, u32[]{:S(2)}) %collective-permute-start.4) | collective-permute-done | bytes 917536 | tf_op jit(solution)/shard_map/ppermute | solution.py:321
  125.5 4.4 %shard_map.55 = (bf16[8,128,512]{2,1,0:T(8,128)(2,1)}, f32[8,512]{1,0:T(8,128)}) custom-call(s32[56]{0:T(128)} %add.87.source_ref, s32[4]{0:T(128)} %pad_add_fusion.slices_ref, s32[8]{0:T(128)} %get-tuple-element.68.index_ref, s32[8]{0:T(128)} %get-tuple-element.69.valid_ref, bf16[56,128,1024]{2,1,0:T(8,128)(2,1)} %bitcast.58, ...), custom_call_target="tpu_custom_call" | custom-call | tf_op jit(solution)/shard_map/pallas_call | solution.py:141
  153.8 5.8 %all-to-all-start.3 = ((bf16[8,128,512]{2,1,0:T(8,128)(2,1)}), bf16[8,128,512]{2,1,0:T(8,128)(2,1)}, u32[]{:S(2)}, u32[]{:S(2)}) async-start(bf16[8,128,512]{2,1,0:T(8,128)(2,1)} %get-tuple-element.57), calls=%async_computation.3 | async-start | bytes 2097152 | tf_op jit(solution)/shard_map/all_to_all | solution.py:344
  159.5 13.2 %precondition.3 = (bf16[1024,1024]{1,0:T(8,128)(2,1)}, bf16[1024,256]{1,0:T(8,128)(2,1)S(1)}) custom-call(s32[1]{0:T(128)} %constant.77.clone.1.slot_ref, f32[1,1]{1,0:T(1,128)} %bitcast.11.clip_ref, bf16[2,1024,256]{2,1,0:T(8,128)(2,1)S(1)} %bitcast.44, bf16[1024,512]{1,0:T(8,128)(2,1)S(1)} %bitcast.46, bf16[1024,512]{1,0:T(8,128)(2,1)S(1)} %bitcast.47), custom_call_target="tpu_custom_call" | custom-call | flops 6442450944 | bytes 6291456 | tf_op jit(solution)/shard_map/precondition/pallas_call | solution.py:98
  173.6 7.8 %all-to-all-done.3 = bf16[8,128,512]{2,1,0:T(8,128)(2,1)} async-done(((bf16[8,128,512]{2,1,0:T(8,128)(2,1)}), bf16[8,128,512]{2,1,0:T(8,128)(2,1)}, u32[]{:S(2)}, u32[]{:S(2)}) %all-to-all-start.3) | async-done | bytes 1048608 | tf_op jit(solution)/shard_map/all_to_all | solution.py:344
  181.4 4.6 %all-to-all-start.5 = ((bf16[8,128,1024]{2,1,0:T(8,128)(2,1)}), bf16[8,128,1024]{2,1,0:T(8,128)(2,1)}, u32[]{:S(2)}, u32[]{:S(2)}) async-start(bf16[8,128,1024]{2,1,0:T(8,128)(2,1)} %bitcast.17), calls=%async_computation.5 | async-start | bytes 4194304 | tf_op jit(solution)/shard_map/all_to_all | solution.py:357
  186.5 14.7 %precondition.2 = (bf16[1024,1024]{1,0:T(8,128)(2,1)}, bf16[1024,256]{1,0:T(8,128)(2,1)S(1)}) custom-call(s32[1]{0:T(128)} %bitcast.2.slot_ref, f32[1,1]{1,0:T(1,128)} %bitcast.11.clip_ref, bf16[2,1024,256]{2,1,0:T(8,128)(2,1)S(1)} %bitcast.45, bf16[1024,512]{1,0:T(8,128)(2,1)} %bitcast.13.rest_0_, bf16[1024,512]{1,0:T(8,128)(2,1)} %bitcast.14.rest_1_), custom_call_target="tpu_custom_call" | custom-call | flops 6442450944 | bytes 6291456 | tf_op jit(solution)/shard_map/precondition/pallas_call | solution.py:98
  201.3 30.9 %all-to-all-done.5.source_ref = bf16[8,128,1024]{2,1,0:T(8,128)(2,1)} async-done(((bf16[8,128,1024]{2,1,0:T(8,128)(2,1)}), bf16[8,128,1024]{2,1,0:T(8,128)(2,1)}, u32[]{:S(2)}, u32[]{:S(2)}) %all-to-all-start.5) | async-done | bytes 2097184 | tf_op jit(solution)/shard_map/all_to_all | solution.py:357
  232.1 4.5 %all-to-all-start.4 = ((bf16[8,128,1024]{2,1,0:T(8,128)(2,1)}), bf16[8,128,1024]{2,1,0:T(8,128)(2,1)}, u32[]{:S(2)}, u32[]{:S(2)}) async-start(bf16[8,128,1024]{2,1,0:T(8,128)(2,1)} %bitcast.15), calls=%async_computation.4 | async-start | bytes 4194304 | tf_op jit(solution)/shard_map/all_to_all | solution.py:357
  242.9 41.2 %all-to-all-done.4.source_ref = bf16[8,128,1024]{2,1,0:T(8,128)(2,1)} async-done(((bf16[8,128,1024]{2,1,0:T(8,128)(2,1)}), bf16[8,128,1024]{2,1,0:T(8,128)(2,1)}, u32[]{:S(2)}, u32[]{:S(2)}) %all-to-all-start.4) | async-done | bytes 2097184 | tf_op jit(solution)/shard_map/all_to_all | solution.py:357
  (110 shorter events, 55.5 us)
Async XLA Ops:
  7.9 5.4 %collective-permute-start = (bf16[7,128,512]{2,1,0:T(8,128)(2,1)}, bf16[7,128,512]{2,1,0:T(8,128)(2,1)S(1)}, u32[]{:S(2)}, u32[]{:S(2)}) collective-permute-start(bf16[7,128,512]{2,1,0:T(8,128)(2,1)} %pick_blocks.3), channel_id=1, source_target_pairs={{0,1},{1,0},{2,3},{3,2},{4,5},{5,4},{6,7},{7,6},{8,9},{9,8},{10,11... | collective-permute-start | bytes 2752520 | tf_op jit(solution)/shard_map/ppermute | solution.py:319
  12.6 8.0 %collective-permute-start.1 = (bf16[7,128,512]{2,1,0:T(8,128)(2,1)}, bf16[7,128,512]{2,1,0:T(8,128)(2,1)}, u32[]{:S(2)}, u32[]{:S(2)}) collective-permute-start(bf16[7,128,512]{2,1,0:T(8,128)(2,1)} %get-tuple-element.36), channel_id=1, source_target_pairs={{0,1},{1,0},{2,3},{3,2},{4,5},{5,4},{6,7},{7,6},{8,9},{9,8},{10,11... | collective-permute-start | bytes 2752520 | tf_op jit(solution)/shard_map/ppermute | solution.py:319
  12.7 11.4 %collective-permute-start.2 = (bf16[7,128,512]{2,1,0:T(8,128)(2,1)}, bf16[7,128,512]{2,1,0:T(8,128)(2,1)S(1)}, u32[]{:S(2)}, u32[]{:S(2)}) collective-permute-start(bf16[7,128,512]{2,1,0:T(8,128)(2,1)} %get-tuple-element.38), channel_id=1, source_target_pairs={{0,1},{1,0},{2,3},{3,2},{4,5},{5,4},{6,7},{7,6},{8,9},{9,8},{10,11... | collective-permute-start | bytes 2752520 | tf_op jit(solution)/shard_map/ppermute | solution.py:319
  13.2 15.4 %collective-permute-start.3 = (bf16[7,128,512]{2,1,0:T(8,128)(2,1)}, bf16[7,128,512]{2,1,0:T(8,128)(2,1)S(1)}, u32[]{:S(2)}, u32[]{:S(2)}) collective-permute-start(bf16[7,128,512]{2,1,0:T(8,128)(2,1)} %get-tuple-element.40), channel_id=1, source_target_pairs={{0,1},{1,0},{2,3},{3,2},{4,5},{5,4},{6,7},{7,6},{8,9},{9,8},{10,11... | collective-permute-start | bytes 2752520 | tf_op jit(solution)/shard_map/ppermute | solution.py:319
  17.7 23.8 %collective-permute-start.8 = (bf16[7,128,512]{2,1,0:T(8,128)(2,1)}, bf16[7,128,512]{2,1,0:T(8,128)(2,1)S(1)}, u32[]{:S(2)}, u32[]{:S(2)}) collective-permute-start(bf16[7,128,512]{2,1,0:T(8,128)(2,1)} %shard_map.50), channel_id=1, source_target_pairs={{0,2},{1,3},{2,0},{3,1},{4,6},{5,7},{6,4},{7,5},{8,10},{9,11},{10,... | collective-permute-start | bytes 2752520 | tf_op jit(solution)/shard_map/ppermute | solution.py:321
  37.8 3.7 %collective-permute-start.9 = (bf16[7,128,512]{2,1,0:T(8,128)(2,1)}, bf16[7,128,512]{2,1,0:T(8,128)(2,1)S(1)}, u32[]{:S(2)}, u32[]{:S(2)}) collective-permute-start(bf16[7,128,512]{2,1,0:T(8,128)(2,1)} %get-tuple-element.47), channel_id=1, source_target_pairs={{0,1},{1,0},{2,3},{3,2},{4,5},{5,4},{6,7},{7,6},{8,9},{9,8},{10,11... | collective-permute-start | bytes 2752520 | tf_op jit(solution)/shard_map/ppermute | solution.py:326
  47.2 32.8 %all-to-all-start.1 = ((bf16[8,128,512]{2,1,0:T(8,128)(2,1)}), bf16[8,128,512]{2,1,0:T(8,128)(2,1)S(1)}, u32[]{:S(2)}, u32[]{:S(2)}) async-start(bf16[8,128,512]{2,1,0:T(8,128)(2,1)} %get-tuple-element.50), calls=%async_computation.1 | async-start | bytes 2097152 | tf_op jit(solution)/shard_map/all_to_all | solution.py:344
  53.3 21.3 %collective-permute-start.5 = (bf16[7,128,512]{2,1,0:T(8,128)(2,1)S(1)}, bf16[7,128,512]{2,1,0:T(8,128)(2,1)S(1)}, u32[]{:S(2)}, u32[]{:S(2)}) collective-permute-start(bf16[7,128,512]{2,1,0:T(8,128)(2,1)S(1)} %copy-done.4), channel_id=1, source_target_pairs={{0,2},{1,3},{2,0},{3,1},{4,6},{5,7},{6,4},{7,5},{8,10},{9,11},{10,... | collective-permute-start | bytes 2752520 | tf_op jit(solution)/shard_map/ppermute | solution.py:321
  54.9 19.7 %collective-permute-start.6 = (bf16[7,128,512]{2,1,0:T(8,128)(2,1)}, bf16[7,128,512]{2,1,0:T(8,128)(2,1)}, u32[]{:S(2)}, u32[]{:S(2)}) collective-permute-start(bf16[7,128,512]{2,1,0:T(8,128)(2,1)} %get-tuple-element.42), channel_id=1, source_target_pairs={{0,1},{1,0},{2,3},{3,2},{4,5},{5,4},{6,7},{7,6},{8,9},{9,8},{10,11... | collective-permute-start | bytes 2752520 | tf_op jit(solution)/shard_map/ppermute | solution.py:326
  80.0 33.8 %all-to-all-start = ((bf16[8,128,512]{2,1,0:T(8,128)(2,1)}), bf16[8,128,512]{2,1,0:T(8,128)(2,1)S(1)}, u32[]{:S(2)}, u32[]{:S(2)}) async-start(bf16[8,128,512]{2,1,0:T(8,128)(2,1)} %get-tuple-element.43), calls=%async_computation | async-start | bytes 2097152 | tf_op jit(solution)/shard_map/all_to_all | solution.py:344
  85.8 23.5 %collective-permute-start.10 = (bf16[7,128,512]{2,1,0:T(8,128)(2,1)}, bf16[7,128,512]{2,1,0:T(8,128)(2,1)}, u32[]{:S(2)}, u32[]{:S(2)}) collective-permute-start(bf16[7,128,512]{2,1,0:T(8,128)(2,1)} %shard_map.52), channel_id=1, source_target_pairs={{0,2},{1,3},{2,0},{3,1},{4,6},{5,7},{6,4},{7,5},{8,10},{9,11},{10,... | collective-permute-start | bytes 2752520 | tf_op jit(solution)/shard_map/ppermute | solution.py:321
  87.3 22.0 %collective-permute-start.11 = (bf16[7,128,512]{2,1,0:T(8,128)(2,1)}, bf16[7,128,512]{2,1,0:T(8,128)(2,1)}, u32[]{:S(2)}, u32[]{:S(2)}) collective-permute-start(bf16[7,128,512]{2,1,0:T(8,128)(2,1)} %get-tuple-element.52), channel_id=1, source_target_pairs={{0,1},{1,0},{2,3},{3,2},{4,5},{5,4},{6,7},{7,6},{8,9},{9,8},{10,11... | collective-permute-start | bytes 2752520 | tf_op jit(solution)/shard_map/ppermute | solution.py:326
  87.3 38.2 %collective-permute-start.4 = (bf16[7,128,512]{2,1,0:T(8,128)(2,1)S(1)}, bf16[7,128,512]{2,1,0:T(8,128)(2,1)}, u32[]{:S(2)}, u32[]{:S(2)}) collective-permute-start(bf16[7,128,512]{2,1,0:T(8,128)(2,1)S(1)} %copy-done.3), channel_id=1, source_target_pairs={{0,2},{1,3},{2,0},{3,1},{4,6},{5,7},{6,4},{7,5},{8,10},{9,11},{10,... | collective-permute-start | bytes 2752520 | tf_op jit(solution)/shard_map/ppermute | solution.py:321
  87.8 37.7 %collective-permute-start.7 = (bf16[7,128,512]{2,1,0:T(8,128)(2,1)}, bf16[7,128,512]{2,1,0:T(8,128)(2,1)}, u32[]{:S(2)}, u32[]{:S(2)}) collective-permute-start(bf16[7,128,512]{2,1,0:T(8,128)(2,1)} %get-tuple-element.45), channel_id=1, source_target_pairs={{0,1},{1,0},{2,3},{3,2},{4,5},{5,4},{6,7},{7,6},{8,9},{9,8},{10,11... | collective-permute-start | bytes 2752520 | tf_op jit(solution)/shard_map/ppermute | solution.py:326
  113.8 40.0 %all-to-all-start.2 = ((bf16[8,128,512]{2,1,0:T(8,128)(2,1)}), bf16[8,128,512]{2,1,0:T(8,128)(2,1)}, u32[]{:S(2)}, u32[]{:S(2)}) async-start(bf16[8,128,512]{2,1,0:T(8,128)(2,1)} %get-tuple-element.56), calls=%async_computation.2 | async-start | bytes 2097152 | tf_op jit(solution)/shard_map/all_to_all | solution.py:344
  130.0 29.6 %copy-start = (bf16[1,1,2,1024,256]{4,3,2,1,0:T(8,128)(2,1)S(1)}, bf16[1,1,2,1024,256]{4,3,2,1,0:T(8,128)(2,1)}, u32[]{:S(2)}) copy-start(bf16[1,1,2,1024,256]{4,3,2,1,0:T(8,128)(2,1)} %param.4) | copy-start | bytes 3145732
  133.3 1.2 collective-permute-start.12
  134.5 3.6 %collective-permute-start.13 = (f32[8,128]{1,0:T(8,128)S(1)}, f32[8,128]{1,0:T(8,128)S(1)}, u32[]{:S(2)}, u32[]{:S(2)}) collective-permute-start(f32[8,128]{1,0:T(8,128)S(1)} %broadcast_add_fusion.1), channel_id=1, source_target_pairs={{0,2},{1,3},{2,0},{3,1},{4,6},{5,7},{6,4},{7,5},{8,10},{9,11},{10,... | collective-permute-start | bytes 12296 | tf_op jit(solution)/shard_map/ppermute | solution.py:260
  139.3 3.7 %collective-permute-start.14 = (f32[8,128]{1,0:T(8,128)S(1)}, f32[8,128]{1,0:T(8,128)S(1)}, u32[]{:S(2)}, u32[]{:S(2)}) collective-permute-start(f32[8,128]{1,0:T(8,128)S(1)} %broadcast_in_dim.107), channel_id=1, source_target_pairs={{0,4},{4,0},{8,12},{12,8},{16,20},{20,16},{24,28},{28,24},{1,5},{5... | collective-permute-start | bytes 12296 | tf_op jit(solution)/shard_map/ppermute | solution.py:260
  143.6 3.7 %collective-permute-start.15 = (f32[8,128]{1,0:T(8,128)S(1)}, f32[8,128]{1,0:T(8,128)S(1)}, u32[]{:S(2)}, u32[]{:S(2)}) collective-permute-start(f32[8,128]{1,0:T(8,128)S(1)} %broadcast_add_fusion), channel_id=1, source_target_pairs={{0,8},{4,12},{8,0},{12,4},{16,24},{20,28},{24,16},{28,20},{1,9},{5... | collective-permute-start | bytes 12296 | tf_op jit(solution)/shard_map/ppermute | solution.py:260
  148.0 4.6 %collective-permute-start.16 = (f32[8,128]{1,0:T(8,128)S(1)}, f32[8,128]{1,0:T(8,128)S(1)}, u32[]{:S(2)}, u32[]{:S(2)}) collective-permute-start(f32[8,128]{1,0:T(8,128)S(1)} %fusion.13), channel_id=1, source_target_pairs={{0,16},{4,20},{8,24},{12,28},{16,0},{20,4},{24,8},{28,12},{1,17},{... | collective-permute-start | bytes 12296 | tf_op jit(solution)/shard_map/ppermute | solution.py:260
  153.8 27.6 %all-to-all-start.3 = ((bf16[8,128,512]{2,1,0:T(8,128)(2,1)}), bf16[8,128,512]{2,1,0:T(8,128)(2,1)}, u32[]{:S(2)}, u32[]{:S(2)}) async-start(bf16[8,128,512]{2,1,0:T(8,128)(2,1)} %get-tuple-element.57), calls=%async_computation.3 | async-start | bytes 2097152 | tf_op jit(solution)/shard_map/all_to_all | solution.py:344
  181.4 50.7 %all-to-all-start.5 = ((bf16[8,128,1024]{2,1,0:T(8,128)(2,1)}), bf16[8,128,1024]{2,1,0:T(8,128)(2,1)}, u32[]{:S(2)}, u32[]{:S(2)}) async-start(bf16[8,128,1024]{2,1,0:T(8,128)(2,1)} %bitcast.17), calls=%async_computation.5 | async-start | bytes 4194304 | tf_op jit(solution)/shard_map/all_to_all | solution.py:357
  232.1 52.0 %all-to-all-start.4 = ((bf16[8,128,1024]{2,1,0:T(8,128)(2,1)}), bf16[8,128,1024]{2,1,0:T(8,128)(2,1)}, u32[]{:S(2)}, u32[]{:S(2)}) async-start(bf16[8,128,1024]{2,1,0:T(8,128)(2,1)} %bitcast.15), calls=%async_computation.4 | async-start | bytes 4194304 | tf_op jit(solution)/shard_map/all_to_all | solution.py:357
  (15 other events, 49.4 us)
